TPU v7x, 32 devices: a whole 2x2x4 slice. The times are simulated.
32 devices in a mesh: task: 4 (over z), mp: 8 (over y, x, core).
Axes of the slice: x: 2, y: 2, z: 4, core: 2. Of those that a mesh axis runs over, the one named last changes fastest.
Arguments:
- deter: float32 [1024, 4096], P('task', 'mp'), may hold values from -3 to 3
- draws: int32 [4, 32, 1024], P(None, None, 'task'), may hold values from 0 to 31
- actions: int32 [4, 1024], P(None, 'task'), may hold values from 0 to 17
- horizons: int32 [64], replicated, may hold values from 5 to 30, as said below
- offsets: int32 [4, 4], replicated, may hold values from 0 to 3, as said below
- embed_stoch: bfloat16 [1024, 1024], replicated, may hold values from -1 to 1
- embed_act: bfloat16 [18, 1024], replicated, may hold values from -6 to 6
- gru_weight: bfloat16 [5120, 3, 4096], P(None, None, 'mp'), may hold values from -0.078125 to 0.078125
- prior_weight: bfloat16 [4096, 1024], replicated, may hold values from -0.09375 to 0.09375
- logit_weight: bfloat16 [1024, 1024], replicated, may hold values from -0.75 to 0.75
- head_weight: bfloat16 [1024, 2], replicated, may hold values from -0.375 to 0.375
Outputs:
- log_prob: float32 [4, 1024], P(None, 'task')
- reward: float32 [4, 1024], P(None, 'task')
- continuation: float32 [4, 1024], P(None, 'task')
- final_deter: float32 [1024, 4096], P('task', 'mp')
Inputs may be any that keep to these rules, and one draw needn't show every extreme that they name: `horizons`: rows of task k are home rows k * (16) up to (k + 1) * 16 - 1. `offsets`: the 4 numbers of one row are distinct.
All inputs are finite; a program needn't handle non-finite values.
Results may differ from a plain program's by a relative error of at most 0.0045.
Values may be sent and summed in bfloat16 or wider, within the bound.
A program may use at most 128 MiB of HBM per device.

v0:
```python
import jax
import jax.numpy as jnp
from jax import lax
from jax.sharding import PartitionSpec as P

HID = 1024
GROUPS = 32
CLASSES = 32
ACTS = 18
TASKS = 64
BLK_DEV = 4
STEPS = 4
WSTART = 16


def normed_rows(values):
    entries = values.shape[-1]
    average = jnp.sum(values, axis=-1, keepdims=True) / entries
    squares = jnp.sum(values * values, axis=-1, keepdims=True) / entries
    return (values - average) * lax.rsqrt(squares - average * average + 1e-05)


def product(rows_in, weight):
    return jnp.dot(rows_in, weight, preferred_element_type=jnp.float32)


def recurrence(deter, embedded, gate_weight, living, det_full):
    carried = deter
    rows_here, det_share = deter.shape
    lows = []
    for moment in range(STEPS):
        low = carried.astype(jnp.bfloat16)
        gathered = lax.all_gather(low, "mp", axis=1, tiled=True)
        lows.append(gathered)
        joined = jnp.concatenate([embedded[moment], gathered], axis=1)
        parts = [product(joined, gate_weight[part]) for part in range(3)]
        sums = sum((jnp.sum(part, axis=1) for part in parts))
        squares = sum((jnp.sum(part * part, axis=1) for part in parts))
        sums, squares = lax.psum(jnp.stack([sums, squares]), "mp")
        average = sums / (3 * det_full)
        inverse = lax.rsqrt(squares / (3 * det_full) - average * average + 1e-05)
        normed = [(part - average[:, None]) * inverse[:, None] for part in parts]
        reset_gate = jax.nn.sigmoid(normed[0])
        candidate = jnp.tanh(reset_gate * normed[1])
        update = jax.nn.sigmoid(normed[2] - 1.0)
        renewed = update * candidate + (1.0 - update) * carried
        carried = jnp.where(living[moment][:, None] > 0, renewed, carried)
    return (carried, lows)


def on_device(
    deter,
    draws,
    actions,
    horizons,
    offsets,
    embed_stoch,
    embed_act,
    gru_weight,
    prior_weight,
    logit_weight,
    head_weight,
):
    holders = lax.axis_size("task")
    device = lax.axis_index("task")
    shards = lax.axis_size("mp")
    shard_index = lax.axis_index("mp")
    rows_here, det_share = deter.shape
    block_rows = rows_here // BLK_DEV
    per_task = rows_here * holders // TASKS
    own_rows = rows_here // shards
    places = jnp.arange(holders, dtype=jnp.int32)
    classes = jnp.arange(CLASSES, dtype=jnp.int32)
    running = jnp.cumsum(offsets, axis=0) % holders
    packed = jnp.concatenate([draws, actions[:, None]], axis=1).astype(jnp.bfloat16)
    packed = lax.all_gather(packed, "task")
    packed = packed.reshape(holders, STEPS, GROUPS + 1, BLK_DEV, block_rows)
    at_slot = (device + running) % holders
    picked = places[:, None, None] == at_slot[None]
    packed = jnp.sum(
        jnp.where(picked[:, :, None, :, None], packed.astype(jnp.float32), 0.0), axis=0
    ).astype(jnp.int32)
    packed = packed.reshape(STEPS, GROUPS + 1, rows_here)
    draws_home = jnp.transpose(packed[:, :GROUPS], (0, 2, 1))
    hot = (draws_home[:, :, :, None] == classes).astype(jnp.bfloat16)
    hot = hot.reshape(STEPS * rows_here, GROUPS * CLASSES)
    action_hot = (
        packed[:, GROUPS].reshape(-1)[:, None] == jnp.arange(ACTS, dtype=jnp.int32)
    ).astype(jnp.bfloat16)
    embed_pre = product(hot, embed_stoch) + product(action_hot, embed_act)
    embedded = jax.nn.silu(normed_rows(embed_pre)).astype(jnp.bfloat16)
    embedded = embedded.reshape(STEPS, rows_here, HID)
    home_rows = device * rows_here + jnp.arange(rows_here, dtype=jnp.int32)
    task_ids = jnp.arange(TASKS, dtype=jnp.int32)
    horizon_rows = jnp.sum(
        jnp.where((home_rows // per_task)[:, None] == task_ids, horizons, 0), axis=1
    )
    alive = horizon_rows[None] > WSTART + jnp.arange(STEPS, dtype=jnp.int32)[:, None]
    living = alive.astype(jnp.float32)
    gate_weight = jnp.transpose(gru_weight, (1, 0, 2))
    carried, lows = recurrence(deter, embedded, gate_weight, living, det_share * shards)
    target = (device + running[-1]) % holders
    sending = places[:, None] == target[None, :]
    blocks = carried.reshape(BLK_DEV, block_rows, det_share)
    outgoing = jnp.where(sending[:, :, None, None], blocks[None], 0.0).astype(jnp.bfloat16)
    arrived = lax.all_to_all(
        outgoing.reshape(holders * BLK_DEV * block_rows, det_share),
        "task",
        split_axis=0,
        concat_axis=0,
        tiled=True,
    ).reshape(holders, BLK_DEV, block_rows, det_share)
    taking = places[:, None] == ((device - running[-1]) % holders)[None, :]
    final = jnp.sum(
        jnp.where(taking[:, :, None, None], arrived.astype(jnp.float32), 0.0), axis=0
    ).reshape(rows_here, det_share)

    def own(array, axis):
        return lax.dynamic_slice_in_dim(array, shard_index * own_rows, own_rows, axis)

    state_rows = jnp.concatenate([own(low, 0) for low in lows], axis=0)
    hidden = jax.nn.silu(normed_rows(product(state_rows, prior_weight))).astype(jnp.bfloat16)
    raw = product(hidden, logit_weight).reshape(STEPS * own_rows, GROUPS, CLASSES)
    exponent = jnp.exp(5.0 * jnp.tanh(raw / 5.0))
    own_hot = own(draws_home, 1).reshape(STEPS * own_rows, GROUPS)[:, :, None] == classes
    chosen = jnp.sum(jnp.where(own_hot, exponent, 0.0), axis=-1)
    chances = 0.99 * chosen / jnp.sum(exponent, axis=-1) + 0.01 / CLASSES
    log_prob = jnp.sum(jnp.log(chances), axis=-1)
    head_out = product(hidden, head_weight)
    results = jnp.stack([log_prob, head_out[:, 0], jax.nn.sigmoid(head_out[:, 1])])
    results = results.reshape(3, STEPS, own_rows) * own(living, 1)[None]
    spread = lax.all_gather(results, ("task", "mp"))
    spread = spread.reshape(holders, shards, 3, STEPS, own_rows)
    spread = jnp.transpose(spread, (0, 2, 3, 1, 4)).reshape(holders, 3, STEPS, BLK_DEV, block_rows)
    source = (device - running) % holders
    from_home = places[:, None, None] == source[None]
    outs = jnp.sum(jnp.where(from_home[:, None, :, :, None], spread, 0.0), axis=0)
    outs = outs.reshape(3, STEPS, rows_here)
    return (outs[0], outs[1], outs[2], final)


def solution(mesh):
    in_specs = (
        P("task", "mp"),
        P(None, None, "task"),
        P(None, "task"),
        P(),
        P(),
        P(),
        P(),
        P(None, None, "mp"),
        P(),
        P(),
        P(),
    )
    out_specs = (P(None, "task"), P(None, "task"), P(None, "task"), P("task", "mp"))
    return jax.shard_map(
        on_device, mesh=mesh, in_specs=in_specs, out_specs=out_specs, check_vma=False
    )
```

profile of v0, /device:TPU:0, one launch (start us, length us, event | category | flops | bytes accessed | tf_op | source)
XLA Modules:
  0.0 310.5 jit_solution(17363063580489032251)
XLA Ops:
  12.0 15.7 %all_gather.20 = bf16[4,4,33,256]{3,1,2,0:T(4,128)(2,1)S(1)} all-gather(bf16[1,4,33,256]{3,1,2,0:T(4,128)(2,1)S(1)} %pad_maximum_fusion.16), channel_id=1, replica_groups=mesh['task'=4,'mp'=8] {'task'}, dimensions={0}, use_global_device_ids=true | all-gather | bytes 337920 | tf_op jit(solution)/shard_map/all_gather | solution.py:76
  36.5 4.2 %all-gather.5.cloned.1.call-done = bf16[256,4096]{1,0:T(8,128)(2,1)} async-done(((bf16[256,512]{1,0:T(8,128)(2,1)}), bf16[256,4096]{1,0:T(8,128)(2,1)}) %all-gather.5.cloned.1.call-update) | async-done | bytes 2097168 | tf_op jit(solution)/shard_map/all_gather | solution.py:33
  40.7 4.9 %fusion.59 = (f32[256]{0:T(256)S(1)}, f32[256]{0:T(256)S(1)}, f32[256,512]{1,0:T(8,128)S(1)}) fusion(bf16[3,5120,512]{2,1,0:T(8,128)(2,1)} %bitcast.126, bf16[256,4096]{1,0:T(8,128)(2,1)} %all-gather.5.cloned.1.call-done, bf16[256,1024]{1,0:T(8,128)(2,1)S(1)} %copy.60), kind=kOutput, calls=%fused_computation.170 | convolution fusion | flops 1347812864 | bytes 8390656 | tf_op jit(solution)/shard_map/dot_general | solution.py:24
  45.6 4.8 %fusion.58 = (f32[256]{0:T(256)S(1)}, f32[256]{0:T(256)S(1)}, f32[256,512]{1,0:T(8,128)}) fusion(bf16[3,5120,512]{2,1,0:T(8,128)(2,1)} %bitcast.127, bf16[256,4096]{1,0:T(8,128)(2,1)S(1)} %copy-done.5, bf16[256,1024]{1,0:T(8,128)(2,1)S(1)} %copy.60), kind=kOutput, calls=%fused_computation.169 | convolution fusion | flops 1347812864 | bytes 8390656 | tf_op jit(solution)/shard_map/dot_general | solution.py:24
  50.4 4.9 %fusion.60 = (f32[256]{0:T(256)S(1)}, f32[256]{0:T(256)S(1)}, f32[256,512]{1,0:T(8,128)}) fusion(bf16[3,5120,512]{2,1,0:T(8,128)(2,1)} %bitcast.128, bf16[256,4096]{1,0:T(8,128)(2,1)S(1)} %copy-done.5, bf16[256,1024]{1,0:T(8,128)(2,1)S(1)} %copy.60), kind=kOutput, calls=%fused_computation.171 | convolution fusion | flops 1347812864 | bytes 8390656 | tf_op jit(solution)/shard_map/dot_general | solution.py:24
  55.4 13.1 %psum.28 = f32[2,256]{1,0:T(2,128)S(1)} all-reduce(f32[2,256]{1,0:T(2,128)S(1)} %pad_maximum_fusion.17), channel_id=1, replica_groups=mesh['task'=4,'mp'=8] {'mp'}, use_global_device_ids=true, to_apply=%region_11.12 | all-reduce | flops 512 | bytes 4096 | tf_op jit(solution)/shard_map/psum | solution.py:39
  71.3 27.8 %all-gather.7.cloned.1.call-done = bf16[256,4096]{1,0:T(8,128)(2,1)} async-done(((bf16[256,512]{1,0:T(8,128)(2,1)}), bf16[256,4096]{1,0:T(8,128)(2,1)}) %all-gather.7.cloned.1.call-update) | async-done | bytes 2097168 | tf_op jit(solution)/shard_map/all_gather | solution.py:33
  99.1 4.9 %fusion.56 = (f32[256]{0:T(256)S(1)}, f32[256]{0:T(256)S(1)}, f32[256,512]{1,0:T(8,128)S(1)}) fusion(bf16[3,5120,512]{2,1,0:T(8,128)(2,1)} %bitcast.129, bf16[256,4096]{1,0:T(8,128)(2,1)} %all-gather.7.cloned.1.call-done, bf16[256,1024]{1,0:T(8,128)(2,1)S(1)} %copy.61), kind=kOutput, calls=%fused_computation.167 | convolution fusion | flops 1347812864 | bytes 8390656 | tf_op jit(solution)/shard_map/dot_general | solution.py:24
  104.0 4.8 %fusion.55 = (f32[256]{0:T(256)S(1)}, f32[256]{0:T(256)S(1)}, f32[256,512]{1,0:T(8,128)}) fusion(bf16[3,5120,512]{2,1,0:T(8,128)(2,1)} %bitcast.130, bf16[256,4096]{1,0:T(8,128)(2,1)S(1)} %copy-done.6, bf16[256,1024]{1,0:T(8,128)(2,1)S(1)} %copy.61), kind=kOutput, calls=%fused_computation.166 | convolution fusion | flops 1347812864 | bytes 8390656 | tf_op jit(solution)/shard_map/dot_general | solution.py:24
  108.8 4.8 %fusion.57 = (f32[256]{0:T(256)S(1)}, f32[256]{0:T(256)S(1)}, f32[256,512]{1,0:T(8,128)}) fusion(bf16[3,5120,512]{2,1,0:T(8,128)(2,1)} %bitcast.131, bf16[256,4096]{1,0:T(8,128)(2,1)S(1)} %copy-done.6, bf16[256,1024]{1,0:T(8,128)(2,1)S(1)} %copy.61), kind=kOutput, calls=%fused_computation.168 | convolution fusion | flops 1347812864 | bytes 8390656 | tf_op jit(solution)/shard_map/dot_general | solution.py:24
  113.7 13.1 %psum.29 = f32[2,256]{1,0:T(2,128)S(1)} all-reduce(f32[2,256]{1,0:T(2,128)S(1)} %pad_maximum_fusion.18), channel_id=1, replica_groups=mesh['task'=4,'mp'=8] {'mp'}, use_global_device_ids=true, to_apply=%region_18.19 | all-reduce | flops 512 | bytes 4096 | tf_op jit(solution)/shard_map/psum | solution.py:39
  129.4 28.0 %all-gather.9.cloned.1.call-done = bf16[256,4096]{1,0:T(8,128)(2,1)} async-done(((bf16[256,512]{1,0:T(8,128)(2,1)}), bf16[256,4096]{1,0:T(8,128)(2,1)}) %all-gather.9.cloned.1.call-update) | async-done | bytes 2097168 | tf_op jit(solution)/shard_map/all_gather | solution.py:33
  157.4 4.9 %fusion.53 = (f32[256]{0:T(256)S(1)}, f32[256]{0:T(256)S(1)}, f32[256,512]{1,0:T(8,128)S(1)}) fusion(bf16[3,5120,512]{2,1,0:T(8,128)(2,1)} %bitcast.132, bf16[256,4096]{1,0:T(8,128)(2,1)} %all-gather.9.cloned.1.call-done, bf16[256,1024]{1,0:T(8,128)(2,1)S(1)} %copy.62), kind=kOutput, calls=%fused_computation.164 | convolution fusion | flops 1347812864 | bytes 8390656 | tf_op jit(solution)/shard_map/dot_general | solution.py:24
  162.4 4.1 %fusion.52 = (f32[256]{0:T(256)S(1)}, f32[256]{0:T(256)S(1)}, f32[256,512]{1,0:T(8,128)S(1)}) fusion(bf16[3,5120,512]{2,1,0:T(8,128)(2,1)} %bitcast.133, bf16[256,4096]{1,0:T(8,128)(2,1)S(1)} %copy-done.7, bf16[256,1024]{1,0:T(8,128)(2,1)S(1)} %copy.62), kind=kOutput, calls=%fused_computation.163 | convolution fusion | flops 1347812864 | bytes 8390656 | tf_op jit(solution)/shard_map/dot_general | solution.py:24
  166.5 4.8 %fusion.54 = (f32[256]{0:T(256)S(1)}, f32[256]{0:T(256)S(1)}, f32[256,512]{1,0:T(8,128)}) fusion(bf16[3,5120,512]{2,1,0:T(8,128)(2,1)} %bitcast.134, bf16[256,4096]{1,0:T(8,128)(2,1)S(1)} %copy-done.7, bf16[256,1024]{1,0:T(8,128)(2,1)S(1)} %copy.62), kind=kOutput, calls=%fused_computation.165 | convolution fusion | flops 1347812864 | bytes 8390656 | tf_op jit(solution)/shard_map/dot_general | solution.py:24
  171.3 13.1 %psum.30 = f32[2,256]{1,0:T(2,128)S(1)} all-reduce(f32[2,256]{1,0:T(2,128)S(1)} %pad_maximum_fusion.19), channel_id=1, replica_groups=mesh['task'=4,'mp'=8] {'mp'}, use_global_device_ids=true, to_apply=%region_25.26 | all-reduce | flops 512 | bytes 4096 | tf_op jit(solution)/shard_map/psum | solution.py:39
  192.0 22.9 %all-gather.11.cloned.1.call-done = bf16[256,4096]{1,0:T(8,128)(2,1)} async-done(((bf16[256,512]{1,0:T(8,128)(2,1)}), bf16[256,4096]{1,0:T(8,128)(2,1)}) %all-gather.11.cloned.1.call-update) | async-done | bytes 2097168 | tf_op jit(solution)/shard_map/all_gather | solution.py:33
  214.9 4.9 %fusion.49 = (f32[256]{0:T(256)S(1)}, f32[256]{0:T(256)S(1)}, f32[256,512]{1,0:T(8,128)S(1)}) fusion(bf16[3,5120,512]{2,1,0:T(8,128)(2,1)} %bitcast.135, bf16[256,4096]{1,0:T(8,128)(2,1)} %all-gather.11.cloned.1.call-done, bf16[256,1024]{1,0:T(8,128)(2,1)S(1)} %copy.67), kind=kOutput, calls=%fused_computation.160 | convolution fusion | flops 1347812864 | bytes 8390656 | tf_op jit(solution)/shard_map/dot_general | solution.py:24
  219.8 4.1 %fusion.48 = (f32[256]{0:T(256)S(1)}, f32[256]{0:T(256)S(1)}, f32[256,512]{1,0:T(8,128)S(1)}) fusion(bf16[3,5120,512]{2,1,0:T(8,128)(2,1)} %bitcast.136, bf16[256,4096]{1,0:T(8,128)(2,1)S(1)} %copy-done.8, bf16[256,1024]{1,0:T(8,128)(2,1)S(1)} %copy.67), kind=kOutput, calls=%fused_computation.159 | convolution fusion | flops 1347812864 | bytes 8390656 | tf_op jit(solution)/shard_map/dot_general | solution.py:24
  224.0 4.1 %fusion.50 = (f32[256]{0:T(256)S(1)}, f32[256]{0:T(256)S(1)}, f32[256,512]{1,0:T(8,128)S(1)}) fusion(bf16[3,5120,512]{2,1,0:T(8,128)(2,1)} %bitcast.137, bf16[256,4096]{1,0:T(8,128)(2,1)S(1)} %copy-done.8, bf16[256,1024]{1,0:T(8,128)(2,1)S(1)} %copy.67), kind=kOutput, calls=%fused_computation.161 | convolution fusion | flops 1347812864 | bytes 8390656 | tf_op jit(solution)/shard_map/dot_general | solution.py:24
  228.1 13.3 %psum.31 = f32[2,256]{1,0:T(2,128)S(1)} all-reduce(f32[2,256]{1,0:T(2,128)S(1)} %pad_maximum_fusion.20), channel_id=1, replica_groups=mesh['task'=4,'mp'=8] {'mp'}, use_global_device_ids=true, to_apply=%region_38.39 | all-reduce | flops 512 | bytes 4096 | tf_op jit(solution)/shard_map/psum | solution.py:39
  243.1 4.6 %all-to-all-start = ((bf16[4,256,512]{2,1,0:T(8,128)(2,1)}), bf16[4,256,512]{2,1,0:T(8,128)(2,1)S(1)}, u32[]{:S(2)}, u32[]{:S(2)}) async-start(bf16[4,256,512]{2,1,0:T(8,128)(2,1)} %select_convert_fusion), calls=%async_computation | async-start | bytes 2097152 | tf_op jit(solution)/shard_map/all_to_all | solution.py:106
  248.7 5.1 %fusion.51 = (f32[128]{0:T(128)S(1)}, f32[128]{0:T(128)S(1)}, f32[128,1024]{1,0:T(8,128)S(1)}) fusion(bf16[4096,1024]{1,0:T(8,128)(2,1)} %param.19, bf16[32,4096]{1,0:T(8,128)(2,1)S(1)} %constant_dynamic-slice_fusion.1, bf16[32,4096]{1,0:T(8,128)(2,1)} %constant_dynamic-slice_fusion.2, bf16[32,4096]{1,0:T(8,128)(2,1)} %constant_dynamic-slice_fusion.3, ...), kind=kOutput, calls=%fused_computation.162 | convolution fusion | flops 1078329088 | bytes 9962496 | tf_op jit(solution)/shard_map/dot_general | solution.py:24
  260.8 40.0 %all_gather.25 = f32[32,3,4,32]{3,2,1,0:T(4,128)S(1)} all-gather(f32[1,3,4,32]{3,2,1,0:T(4,128)S(1)} %maximum_multiply_fusion), channel_id=1, replica_groups=mesh['task'=4,'mp'=8] {'task','mp'}, dimensions={0}, use_global_device_ids=true | all-gather | bytes 50688 | tf_op jit(solution)/shard_map/all_gather | solution.py:132
  (128 shorter events, 39.4 us)
Async XLA Ops:
  7.2 22.4 %copy-start = (bf16[1024,1024]{1,0:T(8,128)(2,1)S(1)}, bf16[1024,1024]{1,0:T(8,128)(2,1)}, u32[]{:S(2)}) copy-start(bf16[1024,1024]{1,0:T(8,128)(2,1)} %param.16) | copy-start | bytes 6291460
  7.2 33.5 %all-gather.5.cloned.1.call-start = ((), (), s32[]{:S(2)}) async-start(), calls=%async_computation.1 | async-start | bytes 2359296 | tf_op jit(solution)/shard_map/all_gather | solution.py:33
  9.2 89.9 %all-gather.7.cloned.1.call-start = ((), (), s32[]{:S(2)}) async-start(), calls=%async_computation.2 | async-start | bytes 2359296 | tf_op jit(solution)/shard_map/all_gather | solution.py:33
  29.6 2.6 copy-start.4
  35.1 1.2 copy-start.10
  40.7 4.9 %copy-start.5 = (bf16[256,4096]{1,0:T(8,128)(2,1)S(1)}, bf16[256,4096]{1,0:T(8,128)(2,1)}, u32[]{:S(2)}) copy-start(bf16[256,4096]{1,0:T(8,128)(2,1)} %all-gather.5.cloned.1.call-done) | copy-start | bytes 6291460
  50.4 18.0 %copy-start.2 = (f32[256,512]{1,0:T(8,128)S(1)}, f32[256,512]{1,0:T(8,128)}, u32[]{:S(2)}) copy-start(f32[256,512]{1,0:T(8,128)} %param.11) | copy-start | bytes 1572868
  50.4 20.7 %copy-start.3 = (bf16[256,1024]{0,1:T(8,128)(2,1)S(1)}, bf16[256,1024]{0,1:T(8,128)(2,1)}, u32[]{:S(2)}) copy-start(bf16[256,1024]{0,1:T(8,128)(2,1)} %get-tuple-element.50) | copy-start | bytes 1572868
  70.9 86.6 %all-gather.9.cloned.1.call-start = ((), (), s32[]{:S(2)}) async-start(), calls=%async_computation.3 | async-start | bytes 2359296 | tf_op jit(solution)/shard_map/all_gather | solution.py:33
  99.1 4.9 %copy-start.6 = (bf16[256,4096]{1,0:T(8,128)(2,1)S(1)}, bf16[256,4096]{1,0:T(8,128)(2,1)}, u32[]{:S(2)}) copy-start(bf16[256,4096]{1,0:T(8,128)(2,1)} %all-gather.7.cloned.1.call-done) | copy-start | bytes 6291460
  129.2 85.7 %all-gather.11.cloned.1.call-start = ((), (), s32[]{:S(2)}) async-start(), calls=%async_computation.4 | async-start | bytes 2359296 | tf_op jit(solution)/shard_map/all_gather | solution.py:33
  157.4 4.9 %copy-start.7 = (bf16[256,4096]{1,0:T(8,128)(2,1)S(1)}, bf16[256,4096]{1,0:T(8,128)(2,1)}, u32[]{:S(2)}) copy-start(bf16[256,4096]{1,0:T(8,128)(2,1)} %all-gather.9.cloned.1.call-done) | copy-start | bytes 6291460
  214.9 4.9 %copy-start.8 = (bf16[256,4096]{1,0:T(8,128)(2,1)S(1)}, bf16[256,4096]{1,0:T(8,128)(2,1)}, u32[]{:S(2)}) copy-start(bf16[256,4096]{1,0:T(8,128)(2,1)} %all-gather.11.cloned.1.call-done) | copy-start | bytes 6291460
  243.1 59.8 %all-to-all-start = ((bf16[4,256,512]{2,1,0:T(8,128)(2,1)}), bf16[4,256,512]{2,1,0:T(8,128)(2,1)S(1)}, u32[]{:S(2)}, u32[]{:S(2)}) async-start(bf16[4,256,512]{2,1,0:T(8,128)(2,1)} %select_convert_fusion), calls=%async_computation | async-start | bytes 2097152 | tf_op jit(solution)/shard_map/all_to_all | solution.py:106
  248.7 5.4 %copy-start.9 = (bf16[1024,2]{0,1:T(2,128)(2,1)S(1)}, bf16[1024,2]{0,1:T(2,128)(2,1)}, u32[]{:S(2)}) copy-start(bf16[1024,2]{0,1:T(2,128)(2,1)} %param.21) | copy-start | bytes 12292
  248.7 55.3 %copy-start.1 = (bf16[1024,1024]{1,0:T(8,128)(2,1)S(1)}, bf16[1024,1024]{1,0:T(8,128)(2,1)}, u32[]{:S(2)}) copy-start(bf16[1024,1024]{1,0:T(8,128)(2,1)} %param.16) | copy-start | bytes 6291460
Sparse Core Ops, SparseCore 0:
  9.9 30.8 all-gather.4
  71.0 28.0 all-gather.6
  129.3 28.0 all-gather.8
  186.8 28.0 all-gather.10
where the time goes:
time: 312 us; the launch traced here: 311 us
  blocking collectives  108 us (35%)
  waiting for transfers between devices  83 us (27%)
  matrix products  68.2 us (22%)
  other arithmetic  17.7 us (6%)
  local copies, waits for them, and re-layouts  14.2 us (5%)
  between operations  14.2 us (5%)
  starting transfers between devices  4.94 us (2%)
    all_gather x4, waiting for transfers between devices, recurrence(): gathered = lax.all_gather(low, 'mp', axis=1, tiled=True)  83 us
    dot_general x17, matrix products, product(): return jnp.dot(rows_in, weight, preferred_element_type=jnp.float32)  68.2 us
    psum x4, blocking collectives, recurrence(): sums, squares = lax.psum(jnp.stack([sums, squares]), 'mp')  52.6 us
    all_gather x1, blocking collectives, on_device(): spread = lax.all_gather(results, ('task', 'mp'))  40 us
    all_gather x1, blocking collectives, on_device(): packed = lax.all_gather(packed, 'task')  15.7 us
    convert_element_type x4, other arithmetic, recurrence(): low = carried.astype(jnp.bfloat16)  8.9 us
  transfers between devices with their start and end apart: 5, of which 4 were waited for; matrix products, arithmetic and copies ran while one was open for 10% of the time, Pallas kernels for 0%

commit v1 on v0

--- a/solution.py
+++ b/solution.py
@@ -30,7 +30,14 @@
     lows = []
     for moment in range(STEPS):
         low = carried.astype(jnp.bfloat16)
-        gathered = lax.all_gather(low, "mp", axis=1, tiled=True)
+        ring = [low]
+        for hop in range(7):
+            ring.append(lax.ppermute(ring[-1], "mp", [(dev, (dev + 1) % 8) for dev in range(8)]))
+        gathered = jnp.roll(
+            jnp.concatenate(ring[::-1], axis=1),
+            (lax.axis_index("mp") + 1) * ring[0].shape[1],
+            axis=1,
+        )
         lows.append(gathered)
         joined = jnp.concatenate([embedded[moment], gathered], axis=1)
         parts = [product(joined, gate_weight[part]) for part in range(3)]

time: 312 us -> 415 us (1.33); the launches traced: 311 us -> 407 us
  waiting for transfers between devices: 83 us -> 164 us
  local copies, waits for them, and re-layouts: 14.2 us -> 32.9 us
  between operations: 14.2 us -> 1.83 us
  other arithmetic: 17.7 us -> 28.4 us
  blocking collectives: 108 us -> 103 us
    ppermute x0 -> x28, waiting for transfers between devices: none -> 164 us  [recurrence(): lax.ppermute(ring[-1], 'mp', [(dev, (dev + 1) % 8) for dev in range(8)])]
    all_gather x4 -> x0, waiting for transfers between devices: 83 us -> none  [recurrence(): gathered = lax.all_gather(low, 'mp', axis=1, tiled=True)]
    unnamed x24 -> x112, local copies, waits for them, and re-layouts: 1.12 us -> 19.7 us
    concatenate x0 -> x7, other arithmetic: none -> 8.41 us  [the longest x6 8.37 us: recurrence(): jnp.roll(jnp.concatenate(ring[::-1], axis=1), (lax.axis_index('mp') + 1)...]
    psum x4, blocking collectives: 52.6 us -> 47.2 us  [recurrence(): sums, squares = lax.psum(jnp.stack([sums, squares]), 'mp')]
    dynamic_slice x7 -> x3, local copies, waits for them, and re-layouts: 5.51 us -> 0.21 us  [own(): lax.dynamic_slice_in_dim(array, shard_index * own_rows, own_rows, axis)]
    slice x5, local copies, waits for them, and re-layouts: 1.75 us -> 5.97 us  [recurrence(): joined = jnp.concatenate([embedded[moment], gathered], axis=1)]
  transfers between devices with their start and end apart: 5 -> 29, of which waited for: 4 -> 27; matrix products, arithmetic and copies ran while one was open for 10% -> 9% of each run, Pallas kernels for 0% -> 0%
where the time goes in v1:
time: 415 us; the launch traced here: 407 us
  waiting for transfers between devices  164 us (40%)
  blocking collectives  103 us (25%)
  matrix products  69.9 us (17%)
  local copies, waits for them, and re-layouts  32.9 us (8%)
  other arithmetic  28.4 us (7%)
  starting transfers between devices  6.15 us (1%)
    ppermute x28, waiting for transfers between devices, recurrence(): lax.ppermute(ring[-1], 'mp', [(dev, (dev + 1) % 8) for dev in range(8)])  164 us
    dot_general x17, matrix products, product(): return jnp.dot(rows_in, weight, preferred_element_type=jnp.float32)  69.9 us
    psum x4, blocking collectives, recurrence(): sums, squares = lax.psum(jnp.stack([sums, squares]), 'mp')  47.2 us
    all_gather x1, blocking collectives, on_device(): spread = lax.all_gather(results, ('task', 'mp'))  40.5 us
    unnamed x112, local copies, waits for them, and re-layouts  19.7 us
    all_gather x1, blocking collectives, on_device(): packed = lax.all_gather(packed, 'task')  15.8 us
    concatenate x6, other arithmetic, recurrence(): jnp.roll(jnp.concatenate(ring[::-1], axis=1), (lax.axis_index('mp') + 1)...  8.37 us
  transfers between devices with their start and end apart: 29, of which 27 were waited for; matrix products, arithmetic and copies ran while one was open for 9% of the time, Pallas kernels for 0%

profile of v1, /device:TPU:0, one launch (start us, length us, event | category | flops | bytes accessed | tf_op | source)
XLA Modules:
  0.0 406.9 jit_solution(15461450892630545155)
XLA Ops:
  5.1 15.8 %all_gather.8 = bf16[4,4,33,256]{3,1,2,0:T(4,128)(2,1)S(1)} all-gather(bf16[1,4,33,256]{3,1,2,0:T(4,128)(2,1)S(1)} %pad_maximum_fusion.16), channel_id=1, replica_groups=mesh['task'=4,'mp'=8] {'task'}, dimensions={0}, use_global_device_ids=true | all-gather | bytes 337920 | tf_op jit(solution)/shard_map/all_gather | solution.py:83
  84.5 11.8 %psum.28 = f32[2,256]{1,0:T(2,128)S(1)} all-reduce(f32[2,256]{1,0:T(2,128)S(1)} %pad_maximum_fusion.17), channel_id=1, replica_groups=mesh['task'=4,'mp'=8] {'mp'}, use_global_device_ids=true, to_apply=%region_11.13 | all-reduce | flops 512 | bytes 4096 | tf_op jit(solution)/shard_map/psum | solution.py:46
  98.9 6.7 %collective-permute-done.7 = bf16[256,512]{1,0:T(8,128)(2,1)S(1)} collective-permute-done((bf16[256,512]{1,0:T(8,128)(2,1)S(1)}, bf16[256,512]{1,0:T(8,128)(2,1)S(1)}, u32[]{:S(2)}, u32[]{:S(2)}) %collective-permute-start.7) | collective-permute-done | bytes 262176 | tf_op jit(solution)/shard_map/ppermute | solution.py:35
  105.6 6.7 %collective-permute-done.8 = bf16[256,512]{1,0:T(8,128)(2,1)S(1)} collective-permute-done((bf16[256,512]{1,0:T(8,128)(2,1)S(1)}, bf16[256,512]{1,0:T(8,128)(2,1)S(1)}, u32[]{:S(2)}, u32[]{:S(2)}) %collective-permute-start.8) | collective-permute-done | bytes 262176 | tf_op jit(solution)/shard_map/ppermute | solution.py:35
  112.3 6.7 %collective-permute-done.9 = bf16[256,512]{1,0:T(8,128)(2,1)S(1)} collective-permute-done((bf16[256,512]{1,0:T(8,128)(2,1)S(1)}, bf16[256,512]{1,0:T(8,128)(2,1)S(1)}, u32[]{:S(2)}, u32[]{:S(2)}) %collective-permute-start.9) | collective-permute-done | bytes 262176 | tf_op jit(solution)/shard_map/ppermute | solution.py:35
  119.0 6.7 %collective-permute-done.10 = bf16[256,512]{1,0:T(8,128)(2,1)S(1)} collective-permute-done((bf16[256,512]{1,0:T(8,128)(2,1)S(1)}, bf16[256,512]{1,0:T(8,128)(2,1)S(1)}, u32[]{:S(2)}, u32[]{:S(2)}) %collective-permute-start.10) | collective-permute-done | bytes 262176 | tf_op jit(solution)/shard_map/ppermute | solution.py:35
  125.7 6.7 %collective-permute-done.11 = bf16[256,512]{1,0:T(8,128)(2,1)S(1)} collective-permute-done((bf16[256,512]{1,0:T(8,128)(2,1)S(1)}, bf16[256,512]{1,0:T(8,128)(2,1)S(1)}, u32[]{:S(2)}, u32[]{:S(2)}) %collective-permute-start.11) | collective-permute-done | bytes 262176 | tf_op jit(solution)/shard_map/ppermute | solution.py:35
  132.4 6.8 %collective-permute-done.12 = bf16[256,512]{1,0:T(8,128)(2,1)} collective-permute-done((bf16[256,512]{1,0:T(8,128)(2,1)S(1)}, bf16[256,512]{1,0:T(8,128)(2,1)}, u32[]{:S(2)}, u32[]{:S(2)}) %collective-permute-start.12) | collective-permute-done | bytes 262176 | tf_op jit(solution)/shard_map/ppermute | solution.py:35
  139.5 6.7 %collective-permute-done.13 = bf16[256,512]{1,0:T(8,128)(2,1)} collective-permute-done((bf16[256,512]{1,0:T(8,128)(2,1)}, bf16[256,512]{1,0:T(8,128)(2,1)}, u32[]{:S(2)}, u32[]{:S(2)}) %collective-permute-start.13) | collective-permute-done | bytes 262176 | tf_op jit(solution)/shard_map/ppermute | solution.py:35
  167.1 11.8 %psum.29 = f32[2,256]{1,0:T(2,128)S(1)} all-reduce(f32[2,256]{1,0:T(2,128)S(1)} %pad_maximum_fusion.18), channel_id=1, replica_groups=mesh['task'=4,'mp'=8] {'mp'}, use_global_device_ids=true, to_apply=%region_18.20 | all-reduce | flops 512 | bytes 4096 | tf_op jit(solution)/shard_map/psum | solution.py:46
  180.9 6.7 %collective-permute-done.14 = bf16[256,512]{1,0:T(8,128)(2,1)S(1)} collective-permute-done((bf16[256,512]{1,0:T(8,128)(2,1)S(1)}, bf16[256,512]{1,0:T(8,128)(2,1)S(1)}, u32[]{:S(2)}, u32[]{:S(2)}) %collective-permute-start.14) | collective-permute-done | bytes 262176 | tf_op jit(solution)/shard_map/ppermute | solution.py:35
  187.5 6.7 %collective-permute-done.15 = bf16[256,512]{1,0:T(8,128)(2,1)S(1)} collective-permute-done((bf16[256,512]{1,0:T(8,128)(2,1)S(1)}, bf16[256,512]{1,0:T(8,128)(2,1)S(1)}, u32[]{:S(2)}, u32[]{:S(2)}) %collective-permute-start.15) | collective-permute-done | bytes 262176 | tf_op jit(solution)/shard_map/ppermute | solution.py:35
  194.2 6.7 %collective-permute-done.16 = bf16[256,512]{1,0:T(8,128)(2,1)S(1)} collective-permute-done((bf16[256,512]{1,0:T(8,128)(2,1)S(1)}, bf16[256,512]{1,0:T(8,128)(2,1)S(1)}, u32[]{:S(2)}, u32[]{:S(2)}) %collective-permute-start.16) | collective-permute-done | bytes 262176 | tf_op jit(solution)/shard_map/ppermute | solution.py:35
  200.9 6.7 %collective-permute-done.17 = bf16[256,512]{1,0:T(8,128)(2,1)S(1)} collective-permute-done((bf16[256,512]{1,0:T(8,128)(2,1)S(1)}, bf16[256,512]{1,0:T(8,128)(2,1)S(1)}, u32[]{:S(2)}, u32[]{:S(2)}) %collective-permute-start.17) | collective-permute-done | bytes 262176 | tf_op jit(solution)/shard_map/ppermute | solution.py:35
  207.6 6.7 %collective-permute-done.18 = bf16[256,512]{1,0:T(8,128)(2,1)S(1)} collective-permute-done((bf16[256,512]{1,0:T(8,128)(2,1)S(1)}, bf16[256,512]{1,0:T(8,128)(2,1)S(1)}, u32[]{:S(2)}, u32[]{:S(2)}) %collective-permute-start.18) | collective-permute-done | bytes 262176 | tf_op jit(solution)/shard_map/ppermute | solution.py:35
  214.3 6.8 %collective-permute-done.19 = bf16[256,512]{1,0:T(8,128)(2,1)} collective-permute-done((bf16[256,512]{1,0:T(8,128)(2,1)S(1)}, bf16[256,512]{1,0:T(8,128)(2,1)}, u32[]{:S(2)}, u32[]{:S(2)}) %collective-permute-start.19) | collective-permute-done | bytes 262176 | tf_op jit(solution)/shard_map/ppermute | solution.py:35
  248.9 11.8 %psum.30 = f32[2,256]{1,0:T(2,128)S(1)} all-reduce(f32[2,256]{1,0:T(2,128)S(1)} %pad_maximum_fusion.19), channel_id=1, replica_groups=mesh['task'=4,'mp'=8] {'mp'}, use_global_device_ids=true, to_apply=%region_25.27 | all-reduce | flops 512 | bytes 4096 | tf_op jit(solution)/shard_map/psum | solution.py:46
  262.7 6.7 %collective-permute-done.21 = bf16[256,512]{1,0:T(8,128)(2,1)S(1)} collective-permute-done((bf16[256,512]{1,0:T(8,128)(2,1)S(1)}, bf16[256,512]{1,0:T(8,128)(2,1)S(1)}, u32[]{:S(2)}, u32[]{:S(2)}) %collective-permute-start.21) | collective-permute-done | bytes 262176 | tf_op jit(solution)/shard_map/ppermute | solution.py:35
  269.3 6.7 %collective-permute-done.22 = bf16[256,512]{1,0:T(8,128)(2,1)S(1)} collective-permute-done((bf16[256,512]{1,0:T(8,128)(2,1)S(1)}, bf16[256,512]{1,0:T(8,128)(2,1)S(1)}, u32[]{:S(2)}, u32[]{:S(2)}) %collective-permute-start.22) | collective-permute-done | bytes 262176 | tf_op jit(solution)/shard_map/ppermute | solution.py:35
  276.0 6.7 %collective-permute-done.23 = bf16[256,512]{1,0:T(8,128)(2,1)S(1)} collective-permute-done((bf16[256,512]{1,0:T(8,128)(2,1)S(1)}, bf16[256,512]{1,0:T(8,128)(2,1)S(1)}, u32[]{:S(2)}, u32[]{:S(2)}) %collective-permute-start.23) | collective-permute-done | bytes 262176 | tf_op jit(solution)/shard_map/ppermute | solution.py:35
  283.5 6.8 %collective-permute-done.24 = bf16[256,512]{1,0:T(8,128)(2,1)} collective-permute-done((bf16[256,512]{1,0:T(8,128)(2,1)S(1)}, bf16[256,512]{1,0:T(8,128)(2,1)}, u32[]{:S(2)}, u32[]{:S(2)}) %collective-permute-start.24) | collective-permute-done | bytes 262176 | tf_op jit(solution)/shard_map/ppermute | solution.py:35
  290.9 6.4 %collective-permute-done.25 = bf16[256,512]{1,0:T(8,128)(2,1)} collective-permute-done((bf16[256,512]{1,0:T(8,128)(2,1)}, bf16[256,512]{1,0:T(8,128)(2,1)}, u32[]{:S(2)}, u32[]{:S(2)}) %collective-permute-start.25) | collective-permute-done | bytes 262176 | tf_op jit(solution)/shard_map/ppermute | solution.py:35
  331.5 11.8 %psum.31 = f32[2,256]{1,0:T(2,128)S(1)} all-reduce(f32[2,256]{1,0:T(2,128)S(1)} %pad_maximum_fusion.20), channel_id=1, replica_groups=mesh['task'=4,'mp'=8] {'mp'}, use_global_device_ids=true, to_apply=%region_38.40 | all-reduce | flops 512 | bytes 4096 | tf_op jit(solution)/shard_map/psum | solution.py:46
  362.9 40.5 %all_gather.9 = f32[32,3,4,32]{3,2,1,0:T(4,128)S(1)} all-gather(f32[1,3,4,32]{3,2,1,0:T(4,128)S(1)} %maximum_multiply_fusion), channel_id=1, replica_groups=mesh['task'=4,'mp'=8] {'task','mp'}, dimensions={0}, use_global_device_ids=true | all-gather | bytes 50688 | tf_op jit(solution)/shard_map/all_gather | solution.py:139
  (266 shorter events, 181.1 us)
Async XLA Ops:
  1.9 20.9 %collective-permute-start = (bf16[256,512]{1,0:T(8,128)(2,1)S(1)}, bf16[256,512]{1,0:T(8,128)(2,1)S(1)}, u32[]{:S(2)}, u32[]{:S(2)}) collective-permute-start(bf16[256,512]{1,0:T(8,128)(2,1)S(1)} %convert_element_type.50), channel_id=1, source_target_pairs={{0,1},{1,2},{2,3},{3,4},{4,5},{5,6},{6,7},{7,0},{8,9},{9,10},{10,1... | collective-permute-start | bytes 786440 | tf_op jit(solution)/shard_map/ppermute | solution.py:35
  22.8 6.7 %collective-permute-start.1 = (bf16[256,512]{1,0:T(8,128)(2,1)S(1)}, bf16[256,512]{1,0:T(8,128)(2,1)S(1)}, u32[]{:S(2)}, u32[]{:S(2)}) collective-permute-start(bf16[256,512]{1,0:T(8,128)(2,1)S(1)} %collective-permute-done), channel_id=1, source_target_pairs={{0,1},{1,2},{2,3},{3,4},{4,5},{5,6},{6,7},{7,0},{8,9},{9,10},{10,1... | collective-permute-start | bytes 786440 | tf_op jit(solution)/shard_map/ppermute | solution.py:35
  29.6 6.7 %collective-permute-start.2 = (bf16[256,512]{1,0:T(8,128)(2,1)S(1)}, bf16[256,512]{1,0:T(8,128)(2,1)S(1)}, u32[]{:S(2)}, u32[]{:S(2)}) collective-permute-start(bf16[256,512]{1,0:T(8,128)(2,1)S(1)} %collective-permute-done.1), channel_id=1, source_target_pairs={{0,1},{1,2},{2,3},{3,4},{4,5},{5,6},{6,7},{7,0},{8,9},{9,10},{10,1... | collective-permute-start | bytes 786440 | tf_op jit(solution)/shard_map/ppermute | solution.py:35
  36.3 6.7 %collective-permute-start.3 = (bf16[256,512]{1,0:T(8,128)(2,1)S(1)}, bf16[256,512]{1,0:T(8,128)(2,1)S(1)}, u32[]{:S(2)}, u32[]{:S(2)}) collective-permute-start(bf16[256,512]{1,0:T(8,128)(2,1)S(1)} %collective-permute-done.2), channel_id=1, source_target_pairs={{0,1},{1,2},{2,3},{3,4},{4,5},{5,6},{6,7},{7,0},{8,9},{9,10},{10,1... | collective-permute-start | bytes 786440 | tf_op jit(solution)/shard_map/ppermute | solution.py:35
  43.0 6.8 %collective-permute-start.4 = (bf16[256,512]{1,0:T(8,128)(2,1)S(1)}, bf16[256,512]{1,0:T(8,128)(2,1)}, u32[]{:S(2)}, u32[]{:S(2)}) collective-permute-start(bf16[256,512]{1,0:T(8,128)(2,1)S(1)} %collective-permute-done.3), channel_id=1, source_target_pairs={{0,1},{1,2},{2,3},{3,4},{4,5},{5,6},{6,7},{7,0},{8,9},{9,10},{10,1... | collective-permute-start | bytes 786440 | tf_op jit(solution)/shard_map/ppermute | solution.py:35
  49.8 6.9 %collective-permute-start.5 = (bf16[256,512]{1,0:T(8,128)(2,1)}, bf16[256,512]{1,0:T(8,128)(2,1)S(1)}, u32[]{:S(2)}, u32[]{:S(2)}) collective-permute-start(bf16[256,512]{1,0:T(8,128)(2,1)} %collective-permute-done.4), channel_id=1, source_target_pairs={{0,1},{1,2},{2,3},{3,4},{4,5},{5,6},{6,7},{7,0},{8,9},{9,10},{10,1... | collective-permute-start | bytes 786440 | tf_op jit(solution)/shard_map/ppermute | solution.py:35
  56.7 7.1 %collective-permute-start.6 = (bf16[256,512]{1,0:T(8,128)(2,1)S(1)}, bf16[256,512]{1,0:T(8,128)(2,1)S(1)}, u32[]{:S(2)}, u32[]{:S(2)}) collective-permute-start(bf16[256,512]{1,0:T(8,128)(2,1)S(1)} %collective-permute-done.5), channel_id=1, source_target_pairs={{0,1},{1,2},{2,3},{3,4},{4,5},{5,6},{6,7},{7,0},{8,9},{9,10},{10,1... | collective-permute-start | bytes 786440 | tf_op jit(solution)/shard_map/ppermute | solution.py:35
  105.6 6.7 %collective-permute-start.8 = (bf16[256,512]{1,0:T(8,128)(2,1)S(1)}, bf16[256,512]{1,0:T(8,128)(2,1)S(1)}, u32[]{:S(2)}, u32[]{:S(2)}) collective-permute-start(bf16[256,512]{1,0:T(8,128)(2,1)S(1)} %collective-permute-done.7), channel_id=1, source_target_pairs={{0,1},{1,2},{2,3},{3,4},{4,5},{5,6},{6,7},{7,0},{8,9},{9,10},{10,1... | collective-permute-start | bytes 786440 | tf_op jit(solution)/shard_map/ppermute | solution.py:35
  112.3 6.7 %collective-permute-start.9 = (bf16[256,512]{1,0:T(8,128)(2,1)S(1)}, bf16[256,512]{1,0:T(8,128)(2,1)S(1)}, u32[]{:S(2)}, u32[]{:S(2)}) collective-permute-start(bf16[256,512]{1,0:T(8,128)(2,1)S(1)} %collective-permute-done.8), channel_id=1, source_target_pairs={{0,1},{1,2},{2,3},{3,4},{4,5},{5,6},{6,7},{7,0},{8,9},{9,10},{10,1... | collective-permute-start | bytes 786440 | tf_op jit(solution)/shard_map/ppermute | solution.py:35
  119.0 6.7 %collective-permute-start.10 = (bf16[256,512]{1,0:T(8,128)(2,1)S(1)}, bf16[256,512]{1,0:T(8,128)(2,1)S(1)}, u32[]{:S(2)}, u32[]{:S(2)}) collective-permute-start(bf16[256,512]{1,0:T(8,128)(2,1)S(1)} %collective-permute-done.9), channel_id=1, source_target_pairs={{0,1},{1,2},{2,3},{3,4},{4,5},{5,6},{6,7},{7,0},{8,9},{9,10},{10,1... | collective-permute-start | bytes 786440 | tf_op jit(solution)/shard_map/ppermute | solution.py:35
  125.7 6.7 %collective-permute-start.11 = (bf16[256,512]{1,0:T(8,128)(2,1)S(1)}, bf16[256,512]{1,0:T(8,128)(2,1)S(1)}, u32[]{:S(2)}, u32[]{:S(2)}) collective-permute-start(bf16[256,512]{1,0:T(8,128)(2,1)S(1)} %collective-permute-done.10), channel_id=1, source_target_pairs={{0,1},{1,2},{2,3},{3,4},{4,5},{5,6},{6,7},{7,0},{8,9},{9,10},{10,1... | collective-permute-start | bytes 786440 | tf_op jit(solution)/shard_map/ppermute | solution.py:35
  132.4 6.8 %collective-permute-start.12 = (bf16[256,512]{1,0:T(8,128)(2,1)S(1)}, bf16[256,512]{1,0:T(8,128)(2,1)}, u32[]{:S(2)}, u32[]{:S(2)}) collective-permute-start(bf16[256,512]{1,0:T(8,128)(2,1)S(1)} %collective-permute-done.11), channel_id=1, source_target_pairs={{0,1},{1,2},{2,3},{3,4},{4,5},{5,6},{6,7},{7,0},{8,9},{9,10},{10,1... | collective-permute-start | bytes 786440 | tf_op jit(solution)/shard_map/ppermute | solution.py:35
  139.2 7.0 %collective-permute-start.13 = (bf16[256,512]{1,0:T(8,128)(2,1)}, bf16[256,512]{1,0:T(8,128)(2,1)}, u32[]{:S(2)}, u32[]{:S(2)}) collective-permute-start(bf16[256,512]{1,0:T(8,128)(2,1)} %collective-permute-done.12), channel_id=1, source_target_pairs={{0,1},{1,2},{2,3},{3,4},{4,5},{5,6},{6,7},{7,0},{8,9},{9,10},{10,1... | collective-permute-start | bytes 786440 | tf_op jit(solution)/shard_map/ppermute | solution.py:35
  180.8 6.7 %collective-permute-start.14 = (bf16[256,512]{1,0:T(8,128)(2,1)S(1)}, bf16[256,512]{1,0:T(8,128)(2,1)S(1)}, u32[]{:S(2)}, u32[]{:S(2)}) collective-permute-start(bf16[256,512]{1,0:T(8,128)(2,1)S(1)} %get-tuple-element.45), channel_id=1, source_target_pairs={{0,1},{1,2},{2,3},{3,4},{4,5},{5,6},{6,7},{7,0},{8,9},{9,10},{10,1... | collective-permute-start | bytes 786440 | tf_op jit(solution)/shard_map/ppermute | solution.py:35
  194.2 6.7 %collective-permute-start.16 = (bf16[256,512]{1,0:T(8,128)(2,1)S(1)}, bf16[256,512]{1,0:T(8,128)(2,1)S(1)}, u32[]{:S(2)}, u32[]{:S(2)}) collective-permute-start(bf16[256,512]{1,0:T(8,128)(2,1)S(1)} %collective-permute-done.15), channel_id=1, source_target_pairs={{0,1},{1,2},{2,3},{3,4},{4,5},{5,6},{6,7},{7,0},{8,9},{9,10},{10,1... | collective-permute-start | bytes 786440 | tf_op jit(solution)/shard_map/ppermute | solution.py:35
  200.9 6.7 %collective-permute-start.17 = (bf16[256,512]{1,0:T(8,128)(2,1)S(1)}, bf16[256,512]{1,0:T(8,128)(2,1)S(1)}, u32[]{:S(2)}, u32[]{:S(2)}) collective-permute-start(bf16[256,512]{1,0:T(8,128)(2,1)S(1)} %collective-permute-done.16), channel_id=1, source_target_pairs={{0,1},{1,2},{2,3},{3,4},{4,5},{5,6},{6,7},{7,0},{8,9},{9,10},{10,1... | collective-permute-start | bytes 786440 | tf_op jit(solution)/shard_map/ppermute | solution.py:35
  214.3 6.8 %collective-permute-start.19 = (bf16[256,512]{1,0:T(8,128)(2,1)S(1)}, bf16[256,512]{1,0:T(8,128)(2,1)}, u32[]{:S(2)}, u32[]{:S(2)}) collective-permute-start(bf16[256,512]{1,0:T(8,128)(2,1)S(1)} %collective-permute-done.18), channel_id=1, source_target_pairs={{0,1},{1,2},{2,3},{3,4},{4,5},{5,6},{6,7},{7,0},{8,9},{9,10},{10,1... | collective-permute-start | bytes 786440 | tf_op jit(solution)/shard_map/ppermute | solution.py:35
  221.1 7.2 %collective-permute-start.20 = (bf16[256,512]{1,0:T(8,128)(2,1)}, bf16[256,512]{1,0:T(8,128)(2,1)}, u32[]{:S(2)}, u32[]{:S(2)}) collective-permute-start(bf16[256,512]{1,0:T(8,128)(2,1)} %collective-permute-done.19), channel_id=1, source_target_pairs={{0,1},{1,2},{2,3},{3,4},{4,5},{5,6},{6,7},{7,0},{8,9},{9,10},{10,1... | collective-permute-start | bytes 786440 | tf_op jit(solution)/shard_map/ppermute | solution.py:35
  262.6 6.7 %collective-permute-start.21 = (bf16[256,512]{1,0:T(8,128)(2,1)S(1)}, bf16[256,512]{1,0:T(8,128)(2,1)S(1)}, u32[]{:S(2)}, u32[]{:S(2)}) collective-permute-start(bf16[256,512]{1,0:T(8,128)(2,1)S(1)} %get-tuple-element.43), channel_id=1, source_target_pairs={{0,1},{1,2},{2,3},{3,4},{4,5},{5,6},{6,7},{7,0},{8,9},{9,10},{10,1... | collective-permute-start | bytes 786440 | tf_op jit(solution)/shard_map/ppermute | solution.py:35
  283.5 6.8 %collective-permute-start.24 = (bf16[256,512]{1,0:T(8,128)(2,1)S(1)}, bf16[256,512]{1,0:T(8,128)(2,1)}, u32[]{:S(2)}, u32[]{:S(2)}) collective-permute-start(bf16[256,512]{1,0:T(8,128)(2,1)S(1)} %collective-permute-done.23), channel_id=1, source_target_pairs={{0,1},{1,2},{2,3},{3,4},{4,5},{5,6},{6,7},{7,0},{8,9},{9,10},{10,1... | collective-permute-start | bytes 786440 | tf_op jit(solution)/shard_map/ppermute | solution.py:35
  290.3 7.0 %collective-permute-start.25 = (bf16[256,512]{1,0:T(8,128)(2,1)}, bf16[256,512]{1,0:T(8,128)(2,1)}, u32[]{:S(2)}, u32[]{:S(2)}) collective-permute-start(bf16[256,512]{1,0:T(8,128)(2,1)} %collective-permute-done.24), channel_id=1, source_target_pairs={{0,1},{1,2},{2,3},{3,4},{4,5},{5,6},{6,7},{7,0},{8,9},{9,10},{10,1... | collective-permute-start | bytes 786440 | tf_op jit(solution)/shard_map/ppermute | solution.py:35
  297.3 7.0 %collective-permute-start.26 = (bf16[256,512]{1,0:T(8,128)(2,1)}, bf16[256,512]{1,0:T(8,128)(2,1)}, u32[]{:S(2)}, u32[]{:S(2)}) collective-permute-start(bf16[256,512]{1,0:T(8,128)(2,1)} %collective-permute-done.25), channel_id=1, source_target_pairs={{0,1},{1,2},{2,3},{3,4},{4,5},{5,6},{6,7},{7,0},{8,9},{9,10},{10,1... | collective-permute-start | bytes 786440 | tf_op jit(solution)/shard_map/ppermute | solution.py:35
  304.3 7.1 %collective-permute-start.27 = (bf16[256,512]{1,0:T(8,128)(2,1)}, bf16[256,512]{1,0:T(8,128)(2,1)S(1)}, u32[]{:S(2)}, u32[]{:S(2)}) collective-permute-start(bf16[256,512]{1,0:T(8,128)(2,1)} %collective-permute-done.26), channel_id=1, source_target_pairs={{0,1},{1,2},{2,3},{3,4},{4,5},{5,6},{6,7},{7,0},{8,9},{9,10},{10,1... | collective-permute-start | bytes 786440 | tf_op jit(solution)/shard_map/ppermute | solution.py:35
  346.4 59.2 %all-to-all-start = ((bf16[4,256,512]{2,1,0:T(8,128)(2,1)}), bf16[4,256,512]{2,1,0:T(8,128)(2,1)S(1)}, u32[]{:S(2)}, u32[]{:S(2)}) async-start(bf16[4,256,512]{2,1,0:T(8,128)(2,1)} %select_convert_fusion), calls=%async_computation | async-start | bytes 2097152 | tf_op jit(solution)/shard_map/all_to_all | solution.py:113
  (46 other events, 611.7 us)
